TPU v7x, 32 devices: a whole 2x2x4 slice. The times are simulated.
32 devices in a mesh: grp: 2 (over y), slab: 4 (over z), ang: 4 (over x, core).
Axes of the slice: x: 2, y: 2, z: 4, core: 2. Of those that a mesh axis runs over, the one named last changes fastest.
Arguments:
- volume: bfloat16 [16, 256, 1024], P(('grp', 'slab')), parts along dimension 0, may hold values from -6 to 6
- ray_weights: bfloat16 [8, 1024, 1024], P('ang'), may hold values from -0.0625 to 0.0625
- row_offsets: int32 [8, 8], P('ang'), may hold values from 0 to 8
- measured: float32 [16, 256, 1024], P(('grp', 'ang'), 'slab'), parts along dimension 0, may hold values from -6 to 6
- shifts: float32 [16], P(('grp', 'ang')), parts along dimension 0, may hold values from -4 to 4
Outputs:
- updated_volume: bfloat16 [16, 256, 1024], P(('grp', 'slab')), parts along dimension 0
- last_residual: float32 [16, 256, 1024], P(('grp', 'ang'), 'slab'), parts along dimension 0
- shift_slope: float32 [16], P(('grp', 'ang')), parts along dimension 0
There are 2 independent parts, one for each index of `grp`. A program takes and returns all parts, laid end to end along the dimension named above; an argument that names none is the same for every part. Nothing has to cross between parts.
All inputs are finite; a program needn't handle non-finite values.
Results may differ from a plain program's by a relative error of at most 0.006.
Values may be sent and summed in bfloat16 or wider, within the bound.
A program may use at most 128 MiB of HBM per device.

v0:
```python
import math
import jax
import jax.numpy as jnp
from jax import lax
from jax.sharding import PartitionSpec as P

Y = 256
X = 1024
U = 1024
OFF = 8
ROUNDS = 2
step_size = 0.5


def move_down(products, tilt_table):
    base = jnp.zeros((products.shape[1] + OFF, U), jnp.float32)
    placed = jax.vmap(
        lambda block, shift_rows: lax.dynamic_update_slice(base, block, (shift_rows, jnp.int32(0)))
    )(products, tilt_table)
    return jnp.sum(placed, axis=0)


def backproject(extended, tilt_table, ray_weights, band_rows):
    slices_count = tilt_table.shape[1]
    running = jnp.zeros((slices_count * band_rows, X), jnp.float32)
    for angle_index in range(ray_weights.shape[0]):
        source = extended[angle_index]
        picked = jax.vmap(
            lambda shift_rows: lax.dynamic_slice(source, (shift_rows, jnp.int32(0)), (band_rows, U))
        )(tilt_table[angle_index])
        running = running + lax.dot_general(
            picked.reshape(slices_count * band_rows, U),
            ray_weights[angle_index],
            (((1,), (1,)), ((), ())),
            preferred_element_type=jnp.float32,
        )
    return running


def apply_update(current, running):
    partial_value = lax.optimization_barrier(running.reshape(current.shape).astype(jnp.bfloat16))
    partial_wide = partial_value.astype(jnp.float32)
    gradient = lax.psum(partial_wide, "ang")
    renewed = (current.astype(jnp.float32) - step_size * gradient).astype(jnp.bfloat16)
    return renewed


def per_device(volume, ray_weights, row_offsets, measured, shifts):
    angles_here = ray_weights.shape[0]
    band_rows = measured.shape[1]
    highest = lax.Precision.HIGHEST
    numbers = lax.iota(jnp.int32, U)
    turns = numbers[:, None] * numbers[None, :] % U
    radians = turns.astype(jnp.float32) * (2.0 * math.pi / U)
    cosine = jnp.cos(radians)
    sine = jnp.sin(radians)
    signed = jnp.where(numbers <= (U - 1) // 2, numbers, numbers - U)
    omega = signed.astype(jnp.float32) * (2.0 * math.pi / U)
    flat_rows = measured.reshape(angles_here * band_rows, U)
    real_part = jnp.dot(flat_rows, cosine, precision=highest).reshape(angles_here, band_rows, U)
    imag_part = -jnp.dot(flat_rows, sine, precision=highest).reshape(angles_here, band_rows, U)
    phase = omega[None, None, :] * shifts[:, None, None]
    turned_real = real_part * jnp.cos(phase) + imag_part * jnp.sin(phase)
    turned_imag = imag_part * jnp.cos(phase) - real_part * jnp.sin(phase)
    first_half = jnp.concatenate([turned_real, omega * turned_imag], axis=0).reshape(-1, U)
    second_half = jnp.concatenate([turned_imag, -omega * turned_real], axis=0).reshape(-1, U)
    inverse = (
        jnp.dot(first_half, cosine, precision=highest)
        - jnp.dot(second_half, sine, precision=highest)
    ) / U
    inverse = inverse.reshape(2, angles_here, band_rows, U)
    shifted = inverse[0]
    slope_field = inverse[1]
    projection = shifted
    residual = shifted
    current = volume
    slices_here = volume.shape[0]
    tilt_table = lax.dynamic_slice_in_dim(
        row_offsets, lax.axis_index("slab") * slices_here, slices_here, 1
    )
    for round_index in range(ROUNDS):
        flattened = current.reshape(slices_here * Y, X)
        partials = jnp.stack(
            [
                move_down(
                    jnp.dot(
                        flattened, ray_weights[angle_index], preferred_element_type=jnp.float32
                    ).reshape(slices_here, Y, U),
                    tilt_table[angle_index],
                )[:Y]
                for angle_index in range(angles_here)
            ]
        )
        projection = lax.psum_scatter(partials, "slab", scatter_dimension=1, tiled=True)
        residual = projection - shifted
        rounded = residual.astype(jnp.bfloat16)
        gathered = lax.all_gather(rounded, "slab", axis=1, tiled=True)
        extended = jnp.concatenate(
            [gathered, jnp.zeros((angles_here, OFF, U), jnp.bfloat16)], axis=1
        )
        running = backproject(extended, tilt_table, ray_weights, Y)
        current = apply_update(current, running)
    local_dot = jnp.sum(projection * slope_field, axis=(1, 2))
    shift_slope = lax.psum(local_dot, "slab") / math.sqrt(Y * U)
    return (current, residual, shift_slope)


def solution(mesh):
    in_specs = (
        P(("grp", "slab"), None, None),
        P("ang", None, None),
        P("ang", None),
        P(("grp", "ang"), "slab", None),
        P(("grp", "ang")),
    )
    out_specs = (P(("grp", "slab"), None, None), P(("grp", "ang"), "slab", None), P(("grp", "ang")))
    return jax.shard_map(
        per_device, mesh=mesh, in_specs=in_specs, out_specs=out_specs, check_vma=False
    )
```

profile of v0, /device:TPU:1, one launch (start us, length us, event | category | flops | bytes accessed | tf_op | source)
XLA Modules:
  0.0 434.2 jit_solution(13662559025870306911)
XLA Ops:
  7.3 4.6 %fusion.16 = f32[2,256,1024]{2,1,0:T(8,128)} fusion(bf16[2,256,1024]{2,1,0:T(8,128)(2,1)} %param.5, bf16[2,1024,1024]{2,1,0:T(8,128)(2,1)} %param.6), kind=kOutput, calls=%fused_computation.41 | convolution fusion | flops 1073741824 | bytes 5242880 | tf_op jit(solution)/shard_map/dot_general | solution.py:86
  11.9 2.6 fusion.8
  14.8 1.6 broadcast.119.clone.2
  16.4 23.4 %while.12 = (s32[]{:T(128)}, f32[2,264,1024]{2,1,0:T(8,128)}, s32[2,3]{1,0:T(2,128)S(1)}, f32[2,256,1024]{2,1,0:T(8,128)}, s32[]{:T(128)}, /*index=5*/s32[3]{0:T(128)S(1)}, s32[]{:T(128)}) while((s32[]{:T(128)}, f32[2,264,1024]{2,1,0:T(8,128)}, s32[2,3]{1,0:T(2,128)S(1)}, f32[2,256,1024]{2,1,0:T(8,128)}, s32[]{:T(128)}, /*index=5*/s32[3]{0:T(128)S(1)}, ...), condition=%wide.while_cond.4, body=%wide.while_body.4.sunk | while | flops 262163 | bytes 5243051 | solution.py:18
  17.0 2.6 and_reduce_fusion.8
  19.6 3.6 dynamic-slice_select_fusion.8
  23.2 4.9 %dynamic-update-slice.32 = f32[2,264,1024]{2,1,0:T(8,128)} dynamic-update-slice(f32[2,264,1024]{2,1,0:T(8,128)} %get-tuple-element.455, f32[1,256,1024]{2,1,0:T(8,128)S(1)} %dynamic-slice_select_fusion.8, s32[]{:T(128)} %bitcast.154, s32[]{:T(128)} %bitcast.155, s32[]{:T(128)} %constant.18.clone.1..sunk) | dynamic-update-slice | bytes 2097156 | tf_op jit(solution)/shard_map/vmap(vmap())/scatter
  28.7 2.6 and_reduce_fusion.8
  31.3 3.6 dynamic-slice_select_fusion.8
  34.9 4.9 %dynamic-update-slice.32 = f32[2,264,1024]{2,1,0:T(8,128)} dynamic-update-slice(f32[2,264,1024]{2,1,0:T(8,128)} %get-tuple-element.455, f32[1,256,1024]{2,1,0:T(8,128)S(1)} %dynamic-slice_select_fusion.8, s32[]{:T(128)} %bitcast.154, s32[]{:T(128)} %bitcast.155, s32[]{:T(128)} %constant.18.clone.1..sunk) | dynamic-update-slice | bytes 2097156 | tf_op jit(solution)/shard_map/vmap(vmap())/scatter
  39.9 1.6 broadcast.119.clone.1
  41.5 23.9 %while.13 = (s32[]{:T(128)}, f32[2,264,1024]{2,1,0:T(8,128)}, s32[2,3]{1,0:T(2,128)S(1)}, f32[2,256,1024]{2,1,0:T(8,128)}, s32[]{:T(128)}, /*index=5*/s32[3]{0:T(128)S(1)}, s32[]{:T(128)}) while((s32[]{:T(128)}, f32[2,264,1024]{2,1,0:T(8,128)}, s32[2,3]{1,0:T(2,128)S(1)}, f32[2,256,1024]{2,1,0:T(8,128)}, s32[]{:T(128)}, /*index=5*/s32[3]{0:T(128)S(1)}, ...), condition=%wide.while_cond.5, body=%wide.while_body.5.sunk | while | flops 262163 | bytes 5243051 | solution.py:18
  42.2 2.7 and_reduce_fusion.9
  44.9 3.7 dynamic-slice_select_fusion.9
  48.6 5.0 %dynamic-update-slice.33 = f32[2,264,1024]{2,1,0:T(8,128)} dynamic-update-slice(f32[2,264,1024]{2,1,0:T(8,128)} %get-tuple-element.434, f32[1,256,1024]{2,1,0:T(8,128)S(1)} %dynamic-slice_select_fusion.9, s32[]{:T(128)} %bitcast.159, s32[]{:T(128)} %bitcast.160, s32[]{:T(128)} %constant.18.clone.1..sunk.1) | dynamic-update-slice | bytes 2097156 | tf_op jit(solution)/shard_map/vmap(vmap())/scatter
  54.3 2.7 and_reduce_fusion.9
  57.0 3.7 dynamic-slice_select_fusion.9
  60.7 4.8 %dynamic-update-slice.33 = f32[2,264,1024]{2,1,0:T(8,128)} dynamic-update-slice(f32[2,264,1024]{2,1,0:T(8,128)} %get-tuple-element.434, f32[1,256,1024]{2,1,0:T(8,128)S(1)} %dynamic-slice_select_fusion.9, s32[]{:T(128)} %bitcast.159, s32[]{:T(128)} %bitcast.160, s32[]{:T(128)} %constant.18.clone.1..sunk.1) | dynamic-update-slice | bytes 2097156 | tf_op jit(solution)/shard_map/vmap(vmap())/scatter
  65.4 3.0 reduce_sum.45
  68.4 1.2 reduce_sum.46
  69.7 1.7 slice_bitcast_fusion.2
  71.4 1.5 pad_maximum_fusion
  73.6 18.6 %fusion.26 = f32[1024,128]{0,1:T(8,128)S(1)} fusion(f32[128,1024]{1,0:T(8,128)S(1)} %bitcast.174), kind=kOutput, calls=%fused_computation.54 | convolution fusion | flops 1625292800 | bytes 1048576 | tf_op jit(solution)/shard_map/dot_general | solution.py:60
  92.2 18.7 %fusion.50 = f32[1024,128]{0,1:T(8,128)S(1)} fusion(f32[128,1024]{1,0:T(8,128)S(1)} %bitcast.175), kind=kOutput, calls=%fused_computation.67 | convolution fusion | flops 1625423872 | bytes 1048576 | tf_op jit(solution)/shard_map/dot_general | solution.py:61
  111.3 20.2 %fusion.24 = f32[256,1024]{1,0:T(8,128)S(1)} fusion(f32[256,1024]{1,0:T(8,128)S(1)} %bitcast.185), kind=kOutput, calls=%fused_computation.53 | convolution fusion | flops 3235905536 | bytes 2097152 | tf_op jit(solution)/shard_map/dot_general | solution.py:68
  131.5 20.1 %fusion.47 = f32[256,1024]{1,0:T(8,128)S(1)} fusion(f32[256,1024]{1,0:T(8,128)S(1)} %fusion.24, f32[256,1024]{1,0:T(8,128)S(1)} %bitcast.184), kind=kOutput, calls=%fused_computation.66 | convolution fusion | flops 3236429824 | bytes 3145728 | tf_op jit(solution)/shard_map/dot_general | solution.py:69
  151.7 1.8 subtract_convert_fusion.2
  153.8 29.5 %all-gather.3.cloned.1.call-done = bf16[2,256,1024]{2,1,0:T(8,128)(2,1)} async-done(((bf16[2,64,1024]{2,1,0:T(8,128)(2,1)}), bf16[2,256,1024]{2,1,0:T(8,128)(2,1)}) %all-gather.3.cloned.1.call-update) | async-done | bytes 1048592 | tf_op jit(solution)/shard_map/all_gather | solution.py:97
  183.3 1.3 fusion.53
  185.3 4.2 fusion.10
  190.1 4.5 %add_convert_fusion.1 = bf16[512,1024]{1,0:T(8,128)(2,1)} fusion(f32[512,1024]{1,0:T(8,128)} %fusion.10, bf16[512,1024]{1,0:T(8,128)(2,1)S(1)} %bitcast.182, bf16[2,1024,1024]{2,1,0:T(8,128)(2,1)} %param.6), kind=kOutput, calls=%fused_computation.50 | convolution fusion | flops 1074790400 | bytes 6291456 | tf_op jit(solution)/shard_map/dot_general | solution.py:31
  194.6 42.1 %all-reduce.6 = f32[2,256,1024]{2,1,0:T(8,128)S(1)} all-reduce(bf16[2,256,1024]{2,1,0:T(8,128)(2,1)} %bitcast.178), channel_id=1, replica_groups=mesh['grp'=2,'slab'=4,'ang'=4] {'ang'}, use_global_device_ids=true, to_apply=%region_5.6 | all-reduce | flops 524288 | bytes 3145728 | tf_op jit(solution)/shard_map/psum | solution.py:43
  236.6 1.7 subtract_convert_fusion.1
  238.4 0.8 copy-done.10
  239.1 2.6 fusion.14
  241.7 2.6 fusion.6
  244.3 1.6 broadcast.119.clone.3
  245.9 23.4 %while.14 = (s32[]{:T(128)}, f32[2,264,1024]{2,1,0:T(8,128)}, s32[2,3]{1,0:T(2,128)S(1)}, f32[2,256,1024]{2,1,0:T(8,128)}, s32[]{:T(128)}, /*index=5*/s32[3]{0:T(128)S(1)}, s32[]{:T(128)}) while((s32[]{:T(128)}, f32[2,264,1024]{2,1,0:T(8,128)}, s32[2,3]{1,0:T(2,128)S(1)}, f32[2,256,1024]{2,1,0:T(8,128)}, s32[]{:T(128)}, /*index=5*/s32[3]{0:T(128)S(1)}, ...), condition=%wide.while_cond.6, body=%wide.while_body.6.sunk | while | flops 262163 | bytes 5243051 | solution.py:18
  246.5 2.6 and_reduce_fusion.10
  249.1 3.5 dynamic-slice_select_fusion.10
  252.7 5.0 %dynamic-update-slice.34 = f32[2,264,1024]{2,1,0:T(8,128)} dynamic-update-slice(f32[2,264,1024]{2,1,0:T(8,128)} %get-tuple-element.527, f32[1,256,1024]{2,1,0:T(8,128)S(1)} %dynamic-slice_select_fusion.10, s32[]{:T(128)} %bitcast.164, s32[]{:T(128)} %bitcast.165, s32[]{:T(128)} %constant.18.clone.1..sunk.2) | dynamic-update-slice | bytes 2097156 | tf_op jit(solution)/shard_map/vmap(vmap())/scatter
  258.3 2.6 and_reduce_fusion.10
  260.9 3.5 dynamic-slice_select_fusion.10
  264.4 5.0 %dynamic-update-slice.34 = f32[2,264,1024]{2,1,0:T(8,128)} dynamic-update-slice(f32[2,264,1024]{2,1,0:T(8,128)} %get-tuple-element.527, f32[1,256,1024]{2,1,0:T(8,128)S(1)} %dynamic-slice_select_fusion.10, s32[]{:T(128)} %bitcast.164, s32[]{:T(128)} %bitcast.165, s32[]{:T(128)} %constant.18.clone.1..sunk.2) | dynamic-update-slice | bytes 2097156 | tf_op jit(solution)/shard_map/vmap(vmap())/scatter
  269.4 1.9 reduce_sum.47
  271.4 1.6 broadcast.119.clone
  273.0 23.3 %while.15 = (s32[]{:T(128)}, f32[2,264,1024]{2,1,0:T(8,128)}, s32[2,3]{1,0:T(2,128)S(1)}, f32[2,256,1024]{2,1,0:T(8,128)}, s32[]{:T(128)}, /*index=5*/s32[3]{0:T(128)S(1)}, s32[]{:T(128)}) while((s32[]{:T(128)}, f32[2,264,1024]{2,1,0:T(8,128)}, s32[2,3]{1,0:T(2,128)S(1)}, f32[2,256,1024]{2,1,0:T(8,128)}, s32[]{:T(128)}, /*index=5*/s32[3]{0:T(128)S(1)}, ...), condition=%wide.while_cond.7, body=%wide.while_body.7.sunk | while | flops 262163 | bytes 5243051 | solution.py:18
  273.6 2.6 and_reduce_fusion.11
  276.2 3.6 dynamic-slice_select_fusion.11
  279.8 5.0 %dynamic-update-slice.35 = f32[2,264,1024]{2,1,0:T(8,128)} dynamic-update-slice(f32[2,264,1024]{2,1,0:T(8,128)} %get-tuple-element.506, f32[1,256,1024]{2,1,0:T(8,128)S(1)} %dynamic-slice_select_fusion.11, s32[]{:T(128)} %bitcast.169, s32[]{:T(128)} %bitcast.170, s32[]{:T(128)} %constant.18.clone.1..sunk.3) | dynamic-update-slice | bytes 2097156 | tf_op jit(solution)/shard_map/vmap(vmap())/scatter
  285.4 2.6 and_reduce_fusion.11
  288.0 3.5 dynamic-slice_select_fusion.11
  291.5 4.7 %dynamic-update-slice.35 = f32[2,264,1024]{2,1,0:T(8,128)} dynamic-update-slice(f32[2,264,1024]{2,1,0:T(8,128)} %get-tuple-element.506, f32[1,256,1024]{2,1,0:T(8,128)S(1)} %dynamic-slice_select_fusion.11, s32[]{:T(128)} %bitcast.169, s32[]{:T(128)} %bitcast.170, s32[]{:T(128)} %constant.18.clone.1..sunk.3) | dynamic-update-slice | bytes 2097156 | tf_op jit(solution)/shard_map/vmap(vmap())/scatter
  296.3 1.9 reduce_sum.48
  298.3 1.5 pad_maximum_fusion.1
  299.9 42.4 %reduce-scatter.5.cloned.1.call-done = f32[2,64,1024]{2,1,0:T(8,128)} async-done(((f32[2,256,1024]{2,1,0:T(8,128)}), f32[2,64,1024]{2,1,0:T(8,128)}) %reduce-scatter.5.cloned.1.call-update) | async-done | bytes 524304 | tf_op jit(solution)/shard_map/reduce_scatter | solution.py:94
  342.3 2.1 fusion.76
  344.4 8.7 %psum.23 = f32[2]{0:T(128)S(1)} all-reduce(f32[2]{0:T(128)S(1)} %get-tuple-element.189), channel_id=1, replica_groups=mesh['grp'=2,'slab'=4,'ang'=4] {'slab'}, use_global_device_ids=true, to_apply=%region_13.14 | all-reduce | flops 2 | bytes 16 | tf_op jit(solution)/shard_map/psum | solution.py:104
  353.6 18.1 %all-gather.5.cloned.1.call-done = bf16[2,256,1024]{2,1,0:T(8,128)(2,1)} async-done(((bf16[2,64,1024]{2,1,0:T(8,128)(2,1)}), bf16[2,256,1024]{2,1,0:T(8,128)(2,1)}) %all-gather.5.cloned.1.call-update) | async-done | bytes 1048592 | tf_op jit(solution)/shard_map/all_gather | solution.py:97
  371.6 1.3 fusion.55
  373.5 4.2 fusion.12
  378.2 4.5 %add_convert_fusion = bf16[512,1024]{1,0:T(8,128)(2,1)} fusion(f32[512,1024]{1,0:T(8,128)} %fusion.12, bf16[512,1024]{1,0:T(8,128)(2,1)S(1)} %bitcast.180, bf16[2,1024,1024]{2,1,0:T(8,128)(2,1)} %param.6), kind=kOutput, calls=%fused_computation.48 | convolution fusion | flops 1074790400 | bytes 6291456 | tf_op jit(solution)/shard_map/dot_general | solution.py:31
  382.7 42.2 %all-reduce.7 = f32[2,256,1024]{2,1,0:T(8,128)S(1)} all-reduce(bf16[2,256,1024]{2,1,0:T(8,128)(2,1)} %bitcast.179), channel_id=1, replica_groups=mesh['grp'=2,'slab'=4,'ang'=4] {'ang'}, use_global_device_ids=true, to_apply=%region_11.12 | all-reduce | flops 524288 | bytes 3145728 | tf_op jit(solution)/shard_map/psum | solution.py:43
  424.9 2.6 subtract_convert_fusion
  (90 shorter events, 11.5 us)
Async XLA Ops:
  7.2 66.5 %copy-start = (f32[2,64,1024]{2,1,0:T(8,128)S(1)}, f32[2,64,1024]{2,1,0:T(8,128)}, u32[]{:S(2)}) copy-start(f32[2,64,1024]{2,1,0:T(8,128)} %param.8) | copy-start | bytes 1572868
  7.2 144.5 %reduce-scatter.3.cloned.1.call-start = ((), (), s32[]{:S(2)}) async-start(), calls=%async_computation.2 | async-start | bytes 2621440 | tf_op jit(solution)/shard_map/reduce_scatter | solution.py:94
  7.2 4.7 %copy-start.4 = (bf16[2,256,1024]{2,1,0:T(8,128)(2,1)S(1)}, bf16[2,256,1024]{2,1,0:T(8,128)(2,1)}, u32[]{:S(2)}) copy-start(bf16[2,256,1024]{2,1,0:T(8,128)(2,1)} %param.5) | copy-start | bytes 3145732
  7.2 4.7 %copy-start.9 = (bf16[2,1024,1024]{2,1,0:T(8,128)(2,1)S(1)}, bf16[2,1024,1024]{2,1,0:T(8,128)(2,1)}, u32[]{:S(2)}) copy-start(bf16[2,1024,1024]{2,1,0:T(8,128)(2,1)} %param.6) | copy-start | bytes 12582916
  11.9 2.6 copy-start.6
  11.9 2.7 copy-start.7
  14.5 1.9 copy-start.5
  65.4 3.0 copy-start.2
  71.4 2.0 copy-start.8
  72.9 110.4 %all-gather.3.cloned.1.call-start = ((), (), s32[]{:S(2)}) async-start(), calls=%async_computation.3 | async-start | bytes 1310720 | tf_op jit(solution)/shard_map/all_gather | solution.py:97
  153.6 188.7 %reduce-scatter.5.cloned.1.call-start = ((), (), s32[]{:S(2)}) async-start(), calls=%async_computation.4 | async-start | bytes 2621440 | tf_op jit(solution)/shard_map/reduce_scatter | solution.py:94
  236.6 2.5 copy-start.10
  239.1 2.6 copy-start.3
  299.8 71.8 %all-gather.5.cloned.1.call-start = ((), (), s32[]{:S(2)}) async-start(), calls=%async_computation.5 | async-start | bytes 1310720 | tf_op jit(solution)/shard_map/all_gather | solution.py:97
  382.7 44.7 %copy-start.1 = (f32[2,64,1024]{2,1,0:T(8,128)S(1)}, f32[2,64,1024]{2,1,0:T(8,128)}, u32[]{:S(2)}) copy-start(f32[2,64,1024]{2,1,0:T(8,128)} %param.8) | copy-start | bytes 1572868
Sparse Core Ops, SparseCore 0:
  73.0 45.3 reduce-scatter.2
  153.7 29.5 all-gather.2
  299.9 42.2 reduce-scatter.4
  344.5 27.0 all-gather.4
where the time goes:
time: 440 us; the launch traced here: 434 us
  matrix products  107 us (24%)
  blocking collectives  92.9 us (21%)
  waiting for transfers between devices  90 us (20%)
  other arithmetic  70.2 us (16%)
  local copies, waits for them, and re-layouts  58.4 us (13%)
  between operations  14.3 us (3%)
    psum x2, blocking collectives, apply_update(): gradient = lax.psum(partial_wide, 'ang')  84.2 us
    scatter x16, other arithmetic  49.8 us
    all_gather x2, waiting for transfers between devices, per_device(): gathered = lax.all_gather(rounded, 'slab', axis=1, tiled=True)  47.5 us
    scatter x24, local copies, waits for them, and re-layouts  44.2 us
    reduce_scatter x2, waiting for transfers between devices, per_device(): lax.psum_scatter(partials, 'slab', scatter_dimension=1, tiled=True)  42.4 us
    dot_general x1, matrix products, per_device(): jnp.dot(first_half, cosine, precision=highest)  20.2 us
    dot_general x1, matrix products, per_device(): jnp.dot(second_half, sine, precision=highest)  20.1 us
    dot_general x1, matrix products, per_device(): jnp.dot(flat_rows, sine, precision=highest)  18.7 us
  transfers between devices with their start and end apart: 4, of which 3 were waited for; matrix products, arithmetic and copies ran while one was open for 18% of the time, Pallas kernels for 0%

commit v1 on v0

--- a/solution.py
+++ b/solution.py
@@ -40,7 +40,8 @@
 def apply_update(current, running):
     partial_value = lax.optimization_barrier(running.reshape(current.shape).astype(jnp.bfloat16))
     partial_wide = partial_value.astype(jnp.float32)
-    gradient = lax.psum(partial_wide, "ang")
+    blocks = lax.all_gather(partial_wide, "ang", axis=0, tiled=False)
+    gradient = blocks.sum(axis=0)
     renewed = (current.astype(jnp.float32) - step_size * gradient).astype(jnp.bfloat16)
     return renewed
 

time: 440 us -> 485 us (1.10)
  waiting for transfers between devices: 90 us -> 208 us
  blocking collectives: 92.9 us -> 8.5 us
  other arithmetic: 70.2 us -> 82.2 us
    all_gather x0 -> x2, waiting for transfers between devices: none -> 108 us  [apply_update(): blocks = lax.all_gather(partial_wide, 'ang', axis=0, tiled=False)]
    psum x2 -> x0, blocking collectives: 84.2 us -> none  [apply_update(): gradient = lax.psum(partial_wide, 'ang')]
    reduce_sum x0 -> x2, other arithmetic: none -> 9.16 us  [apply_update(): gradient = blocks.sum(axis=0)]
    all_gather x2, waiting for transfers between devices: 47.5 us -> 56.7 us  [per_device(): gathered = lax.all_gather(rounded, 'slab', axis=1, tiled=True)]
  transfers between devices with their start and end apart: 4 -> 6, of which waited for: 3 -> 5; matrix products, arithmetic and copies ran while one was open for 18% -> 16% of each run, Pallas kernels for 0% -> 0%
where the time goes in v1:
time: 485 us; the launch traced here: 479 us
  waiting for transfers between devices  208 us (43%)
  matrix products  105 us (22%)
  other arithmetic  82.2 us (17%)
  local copies, waits for them, and re-layouts  58.6 us (12%)
  between operations  14.7 us (3%)
  blocking collectives  8.5 us (2%)
    all_gather x2, waiting for transfers between devices, apply_update(): blocks = lax.all_gather(partial_wide, 'ang', axis=0, tiled=False)  108 us
    all_gather x2, waiting for transfers between devices, per_device(): gathered = lax.all_gather(rounded, 'slab', axis=1, tiled=True)  56.7 us
    scatter x16, other arithmetic  49.3 us
    scatter x24, local copies, waits for them, and re-layouts  44.4 us
    reduce_scatter x2, waiting for transfers between devices, per_device(): lax.psum_scatter(partials, 'slab', scatter_dimension=1, tiled=True)  43.2 us
    dot_general x1, matrix products, per_device(): jnp.dot(first_half, cosine, precision=highest)  20.2 us
    dot_general x1, matrix products, per_device(): jnp.dot(second_half, sine, precision=highest)  20.1 us
    dot_general x1, matrix products, per_device(): jnp.dot(flat_rows, sine, precision=highest)  18.6 us
  transfers between devices with their start and end apart: 6, of which 5 were waited for; matrix products, arithmetic and copies ran while one was open for 16% of the time, Pallas kernels for 0%

profile of v1, /device:TPU:1, one launch (start us, length us, event | category | flops | bytes accessed | tf_op | source)
XLA Modules:
  0.0 478.8 jit_solution(5865099235029505596)
XLA Ops:
  7.3 4.6 fusion.16
  11.9 2.6 fusion.8
  14.8 1.6 broadcast.119.clone.2
  16.4 24.1 %while.12 = (s32[]{:T(128)}, f32[2,264,1024]{2,1,0:T(8,128)}, s32[2,3]{1,0:T(2,128)S(1)}, f32[2,256,1024]{2,1,0:T(8,128)}, s32[]{:T(128)}, /*index=5*/s32[3]{0:T(128)S(1)}, s32[]{:T(128)}) while((s32[]{:T(128)}, f32[2,264,1024]{2,1,0:T(8,128)}, s32[2,3]{1,0:T(2,128)S(1)}, f32[2,256,1024]{2,1,0:T(8,128)}, s32[]{:T(128)}, /*index=5*/s32[3]{0:T(128)S(1)}, ...), condition=%wide.while_cond.4, body=%wide.while_body.4.sunk | while | flops 262163 | bytes 5243051 | solution.py:18
  17.1 2.6 and_reduce_fusion.8
  19.7 3.7 dynamic-slice_select_fusion.8
  23.4 5.1 %dynamic-update-slice.32 = f32[2,264,1024]{2,1,0:T(8,128)} dynamic-update-slice(f32[2,264,1024]{2,1,0:T(8,128)} %get-tuple-element.487, f32[1,256,1024]{2,1,0:T(8,128)S(1)} %dynamic-slice_select_fusion.8, s32[]{:T(128)} %bitcast.156, s32[]{:T(128)} %bitcast.157, s32[]{:T(128)} %constant.18.clone.1..sunk) | dynamic-update-slice | bytes 2097156 | tf_op jit(solution)/shard_map/vmap(vmap())/scatter
  29.2 2.6 and_reduce_fusion.8
  31.8 3.7 dynamic-slice_select_fusion.8
  35.5 5.1 %dynamic-update-slice.32 = f32[2,264,1024]{2,1,0:T(8,128)} dynamic-update-slice(f32[2,264,1024]{2,1,0:T(8,128)} %get-tuple-element.487, f32[1,256,1024]{2,1,0:T(8,128)S(1)} %dynamic-slice_select_fusion.8, s32[]{:T(128)} %bitcast.156, s32[]{:T(128)} %bitcast.157, s32[]{:T(128)} %constant.18.clone.1..sunk) | dynamic-update-slice | bytes 2097156 | tf_op jit(solution)/shard_map/vmap(vmap())/scatter
  40.7 1.6 broadcast.119.clone.1
  42.3 23.5 %while.13 = (s32[]{:T(128)}, f32[2,264,1024]{2,1,0:T(8,128)}, s32[2,3]{1,0:T(2,128)S(1)}, f32[2,256,1024]{2,1,0:T(8,128)}, s32[]{:T(128)}, /*index=5*/s32[3]{0:T(128)S(1)}, s32[]{:T(128)}) while((s32[]{:T(128)}, f32[2,264,1024]{2,1,0:T(8,128)}, s32[2,3]{1,0:T(2,128)S(1)}, f32[2,256,1024]{2,1,0:T(8,128)}, s32[]{:T(128)}, /*index=5*/s32[3]{0:T(128)S(1)}, ...), condition=%wide.while_cond.5, body=%wide.while_body.5.sunk | while | flops 262163 | bytes 5243051 | solution.py:18
  42.9 2.6 and_reduce_fusion.9
  45.5 3.6 dynamic-slice_select_fusion.9
  49.2 5.0 %dynamic-update-slice.33 = f32[2,264,1024]{2,1,0:T(8,128)} dynamic-update-slice(f32[2,264,1024]{2,1,0:T(8,128)} %get-tuple-element.466, f32[1,256,1024]{2,1,0:T(8,128)S(1)} %dynamic-slice_select_fusion.9, s32[]{:T(128)} %bitcast.161, s32[]{:T(128)} %bitcast.162, s32[]{:T(128)} %constant.18.clone.1..sunk.1) | dynamic-update-slice | bytes 2097156 | tf_op jit(solution)/shard_map/vmap(vmap())/scatter
  54.8 2.6 and_reduce_fusion.9
  57.4 3.6 dynamic-slice_select_fusion.9
  61.0 4.8 dynamic-update-slice.33
  65.8 3.0 reduce_sum.63
  70.0 1.7 slice_bitcast_fusion.2
  71.7 1.5 pad_maximum_fusion
  74.0 18.6 %fusion.26 = f32[1024,128]{0,1:T(8,128)S(1)} fusion(f32[128,1024]{1,0:T(8,128)S(1)} %bitcast.176), kind=kOutput, calls=%fused_computation.54 | convolution fusion | flops 1625292800 | bytes 1048576 | tf_op jit(solution)/shard_map/dot_general | solution.py:61
  92.6 18.6 %fusion.50 = f32[1024,128]{0,1:T(8,128)S(1)} fusion(f32[128,1024]{1,0:T(8,128)S(1)} %bitcast.177), kind=kOutput, calls=%fused_computation.67 | convolution fusion | flops 1625423872 | bytes 1048576 | tf_op jit(solution)/shard_map/dot_general | solution.py:62
  111.7 20.2 %fusion.24 = f32[256,1024]{1,0:T(8,128)S(1)} fusion(f32[256,1024]{1,0:T(8,128)S(1)} %bitcast.189), kind=kOutput, calls=%fused_computation.53 | convolution fusion | flops 3235905536 | bytes 2097152 | tf_op jit(solution)/shard_map/dot_general | solution.py:69
  131.8 20.1 %fusion.47 = f32[256,1024]{1,0:T(8,128)S(1)} fusion(f32[256,1024]{1,0:T(8,128)S(1)} %fusion.24, f32[256,1024]{1,0:T(8,128)S(1)} %bitcast.188), kind=kOutput, calls=%fused_computation.66 | convolution fusion | flops 3236429824 | bytes 3145728 | tf_op jit(solution)/shard_map/dot_general | solution.py:70
  152.1 1.8 subtract_convert_fusion.2
  154.1 29.5 %all-gather.7.cloned.1.call-done = bf16[2,256,1024]{2,1,0:T(8,128)(2,1)} async-done(((bf16[2,64,1024]{2,1,0:T(8,128)(2,1)}), bf16[2,256,1024]{2,1,0:T(8,128)(2,1)}) %all-gather.7.cloned.1.call-update) | async-done | bytes 1048592 | tf_op jit(solution)/shard_map/all_gather | solution.py:98
  185.7 4.2 fusion.10
  190.5 3.5 add_convert_fusion.1
  194.0 1.6 all_gather.32
  195.7 58.6 %all-gather.11.cloned.1.call-done = f32[8,256,1024]{2,1,0:T(8,128)} async-done(((f32[2,256,1024]{2,1,0:T(8,128)}), f32[8,256,1024]{2,1,0:T(8,128)}) %all-gather.11.cloned.1.call-update) | async-done | bytes 8388624 | tf_op jit(solution)/shard_map/all_gather | solution.py:43
  254.3 4.6 reduce_sum.65
  258.9 1.7 subtract_convert_fusion.1
  261.4 2.6 fusion.14
  264.0 2.6 fusion.6
  266.6 1.6 broadcast.119.clone.3
  268.2 23.2 %while.14 = (s32[]{:T(128)}, f32[2,264,1024]{2,1,0:T(8,128)}, s32[2,3]{1,0:T(2,128)S(1)}, f32[2,256,1024]{2,1,0:T(8,128)}, s32[]{:T(128)}, /*index=5*/s32[3]{0:T(128)S(1)}, s32[]{:T(128)}) while((s32[]{:T(128)}, f32[2,264,1024]{2,1,0:T(8,128)}, s32[2,3]{1,0:T(2,128)S(1)}, f32[2,256,1024]{2,1,0:T(8,128)}, s32[]{:T(128)}, /*index=5*/s32[3]{0:T(128)S(1)}, ...), condition=%wide.while_cond.6, body=%wide.while_body.6.sunk | while | flops 262163 | bytes 5243051 | solution.py:18
  268.8 2.5 and_reduce_fusion.10
  271.4 3.5 dynamic-slice_select_fusion.10
  274.9 4.9 %dynamic-update-slice.34 = f32[2,264,1024]{2,1,0:T(8,128)} dynamic-update-slice(f32[2,264,1024]{2,1,0:T(8,128)} %get-tuple-element.559, f32[1,256,1024]{2,1,0:T(8,128)S(1)} %dynamic-slice_select_fusion.10, s32[]{:T(128)} %bitcast.166, s32[]{:T(128)} %bitcast.167, s32[]{:T(128)} %constant.18.clone.1..sunk.2) | dynamic-update-slice | bytes 2097156 | tf_op jit(solution)/shard_map/vmap(vmap())/scatter
  280.5 2.5 and_reduce_fusion.10
  283.0 3.5 dynamic-slice_select_fusion.10
  286.5 4.9 %dynamic-update-slice.34 = f32[2,264,1024]{2,1,0:T(8,128)} dynamic-update-slice(f32[2,264,1024]{2,1,0:T(8,128)} %get-tuple-element.559, f32[1,256,1024]{2,1,0:T(8,128)S(1)} %dynamic-slice_select_fusion.10, s32[]{:T(128)} %bitcast.166, s32[]{:T(128)} %bitcast.167, s32[]{:T(128)} %constant.18.clone.1..sunk.2) | dynamic-update-slice | bytes 2097156 | tf_op jit(solution)/shard_map/vmap(vmap())/scatter
  291.4 1.9 reduce_sum.66
  293.4 1.6 broadcast.119.clone
  295.0 22.9 %while.15 = (s32[]{:T(128)}, f32[2,264,1024]{2,1,0:T(8,128)}, s32[2,3]{1,0:T(2,128)S(1)}, f32[2,256,1024]{2,1,0:T(8,128)}, s32[]{:T(128)}, /*index=5*/s32[3]{0:T(128)S(1)}, s32[]{:T(128)}) while((s32[]{:T(128)}, f32[2,264,1024]{2,1,0:T(8,128)}, s32[2,3]{1,0:T(2,128)S(1)}, f32[2,256,1024]{2,1,0:T(8,128)}, s32[]{:T(128)}, /*index=5*/s32[3]{0:T(128)S(1)}, ...), condition=%wide.while_cond.7, body=%wide.while_body.7.sunk | while | flops 262163 | bytes 5243051 | solution.py:18
  295.7 2.5 and_reduce_fusion.11
  298.3 3.5 dynamic-slice_select_fusion.11
  301.7 4.8 %dynamic-update-slice.35 = f32[2,264,1024]{2,1,0:T(8,128)} dynamic-update-slice(f32[2,264,1024]{2,1,0:T(8,128)} %get-tuple-element.538, f32[1,256,1024]{2,1,0:T(8,128)S(1)} %dynamic-slice_select_fusion.11, s32[]{:T(128)} %bitcast.171, s32[]{:T(128)} %bitcast.172, s32[]{:T(128)} %constant.18.clone.1..sunk.3) | dynamic-update-slice | bytes 2097156 | tf_op jit(solution)/shard_map/vmap(vmap())/scatter
  307.3 2.5 and_reduce_fusion.11
  309.8 3.5 dynamic-slice_select_fusion.11
  313.3 4.6 dynamic-update-slice.35
  317.9 1.9 reduce_sum.67
  319.9 1.5 pad_maximum_fusion.1
  321.5 43.2 %reduce-scatter.5.cloned.1.call-done = f32[2,64,1024]{2,1,0:T(8,128)} async-done(((f32[2,256,1024]{2,1,0:T(8,128)}), f32[2,64,1024]{2,1,0:T(8,128)}) %reduce-scatter.5.cloned.1.call-update) | async-done | bytes 524304 | tf_op jit(solution)/shard_map/reduce_scatter | solution.py:95
  364.7 2.1 fusion.76
  366.9 27.2 %all-gather.9.cloned.1.call-done = bf16[2,256,1024]{2,1,0:T(8,128)(2,1)} async-done(((bf16[2,64,1024]{2,1,0:T(8,128)(2,1)}), bf16[2,256,1024]{2,1,0:T(8,128)(2,1)}) %all-gather.9.cloned.1.call-update) | async-done | bytes 1048592 | tf_op jit(solution)/shard_map/all_gather | solution.py:98
  395.9 4.2 fusion.12
  400.7 3.5 add_convert_fusion
  404.2 1.6 all_gather.33
  405.8 8.5 %psum.7 = f32[2]{0:T(128)S(1)} all-reduce(f32[2]{0:T(128)S(1)} %get-tuple-element.221), channel_id=1, replica_groups=mesh['grp'=2,'slab'=4,'ang'=4] {'slab'}, use_global_device_ids=true, to_apply=%region_13.14 | all-reduce | flops 2 | bytes 16 | tf_op jit(solution)/shard_map/psum | solution.py:105
  414.9 49.7 %all-gather.13.cloned.1.call-done = f32[8,256,1024]{2,1,0:T(8,128)} async-done(((f32[2,256,1024]{2,1,0:T(8,128)}), f32[8,256,1024]{2,1,0:T(8,128)}) %all-gather.13.cloned.1.call-update) | async-done | bytes 8388624 | tf_op jit(solution)/shard_map/all_gather | solution.py:43
  464.5 4.6 reduce_sum.68
  469.1 2.6 subtract_convert_fusion
  (98 shorter events, 16.4 us)
Async XLA Ops:
  7.2 66.8 %copy-start = (f32[2,64,1024]{2,1,0:T(8,128)S(1)}, f32[2,64,1024]{2,1,0:T(8,128)}, u32[]{:S(2)}) copy-start(f32[2,64,1024]{2,1,0:T(8,128)} %param.8) | copy-start | bytes 1572868
  7.2 144.9 %reduce-scatter.3.cloned.1.call-start = ((), (), s32[]{:S(2)}) async-start(), calls=%async_computation.2 | async-start | bytes 2621440 | tf_op jit(solution)/shard_map/reduce_scatter | solution.py:95
  7.2 4.7 copy-start.4
  7.2 4.7 copy-start.9
  11.9 2.7 copy-start.6
  11.9 2.7 copy-start.7
  14.6 1.9 copy-start.5
  65.8 3.0 copy-start.2
  71.7 2.0 copy-start.8
  73.2 110.4 %all-gather.7.cloned.1.call-start = ((), (), s32[]{:S(2)}) async-start(), calls=%async_computation.3 | async-start | bytes 1310720 | tf_op jit(solution)/shard_map/all_gather | solution.py:98
  153.9 100.4 %all-gather.11.cloned.1.call-start = ((), (), s32[]{:S(2)}) async-start(), calls=%async_computation.6 | async-start | bytes 10485760 | tf_op jit(solution)/shard_map/all_gather | solution.py:43
  195.6 169.1 %reduce-scatter.5.cloned.1.call-start = ((), (), s32[]{:S(2)}) async-start(), calls=%async_computation.4 | async-start | bytes 2621440 | tf_op jit(solution)/shard_map/reduce_scatter | solution.py:95
  258.9 2.5 copy-start.10
  261.4 2.6 copy-start.3
  321.5 72.6 %all-gather.9.cloned.1.call-start = ((), (), s32[]{:S(2)}) async-start(), calls=%async_computation.5 | async-start | bytes 1310720 | tf_op jit(solution)/shard_map/all_gather | solution.py:98
  366.8 97.7 %all-gather.13.cloned.1.call-start = ((), (), s32[]{:S(2)}) async-start(), calls=%async_computation.7 | async-start | bytes 10485760 | tf_op jit(solution)/shard_map/all_gather | solution.py:43
  464.5 7.2 %copy-start.1 = (f32[2,64,1024]{2,1,0:T(8,128)S(1)}, f32[2,64,1024]{2,1,0:T(8,128)}, u32[]{:S(2)}) copy-start(f32[2,64,1024]{2,1,0:T(8,128)} %param.8) | copy-start | bytes 1572868
Sparse Core Ops, SparseCore 0:
  73.3 45.3 reduce-scatter.2
  154.0 29.5 all-gather.6
  195.7 58.5 all-gather.10
  321.6 43.0 reduce-scatter.4
  366.9 27.0 all-gather.8
  406.0 58.5 all-gather.12
